TPU v7x, 32 devices: a whole 2x2x4 slice. The times are simulated.
32 devices in a mesh: rep: 2 (over x), dp: 16 (over y, z, core).
Axes of the slice: x: 2, y: 2, z: 4, core: 2. Of those that a mesh axis runs over, the one named last changes fastest.
Arguments:
- x: bfloat16 [32, 2048, 896], P(('rep', 'dp')), parts along dimension 0
- dy: bfloat16 [32, 2048, 896], P(('rep', 'dp')), parts along dimension 0
- w_gate: bfloat16 [2, 896, 2560], replicated
- w_up: bfloat16 [2, 896, 2560], replicated
- w_down: bfloat16 [2, 2560, 896], replicated
- m_w_gate: float32 [2, 896, 2560], replicated
- m_w_up: float32 [2, 896, 2560], replicated
- m_w_down: float32 [2, 2560, 896], replicated
- v_w_gate: float32 [2, 896, 2560], replicated
- v_w_up: float32 [2, 896, 2560], replicated
- v_w_down: float32 [2, 2560, 896], replicated
Outputs:
- output 1: bfloat16 [4, 896, 2560], P('rep'), parts along dimension 0
- output 2: bfloat16 [4, 896, 2560], P('rep'), parts along dimension 0
- output 3: bfloat16 [4, 2560, 896], P('rep'), parts along dimension 0
- output 4: float32 [4, 896, 2560], P('rep'), parts along dimension 0
- output 5: float32 [4, 896, 2560], P('rep'), parts along dimension 0
- output 6: float32 [4, 2560, 896], P('rep'), parts along dimension 0
- output 7: float32 [4, 896, 2560], P('rep'), parts along dimension 0
- output 8: float32 [4, 896, 2560], P('rep'), parts along dimension 0
- output 9: float32 [4, 2560, 896], P('rep'), parts along dimension 0
There are 2 independent parts. A program takes and returns all parts, laid end to end along the dimension named above; an argument that names none is the same for every part.
All inputs are finite; a program needn't handle non-finite values.
Results may differ from a plain program's by a relative error of at most 0.022.
Values are sent between devices in bfloat16 or wider.
A program may use at most 2.5 GiB of HBM per device.

v0:
```python
import jax
import jax.numpy as jnp
from jax import lax
from jax.sharding import PartitionSpec as P

NAMES = ("w_gate", "w_up", "w_down")


def matmul(a, w):
    return jnp.dot(a, w, preferred_element_type=jnp.float32).astype(jnp.bfloat16)


def normed(h):
    wide = h.astype(jnp.float32)
    scale = lax.rsqrt(jnp.mean(wide**2, -1, keepdims=True) + 1e-6)
    return (wide * scale).astype(jnp.bfloat16)


def layer(h, w):
    a = normed(h)
    gate = jnp.dot(a, w["w_gate"], preferred_element_type=jnp.float32)
    up = jnp.dot(a, w["w_up"], preferred_element_type=jnp.float32)
    return h + matmul((jax.nn.silu(gate) * up).astype(jnp.bfloat16), w["w_down"])


def adamw(w, m, v, g):
    m = 0.9 * m + 0.1 * g
    v = 0.95 * v + 0.05 * g * g
    step = m * lax.rsqrt(v + 1e-8) + 0.1 * w
    return (w - 0.02 * step).astype(jnp.bfloat16), m, v


def solution(mesh):
    def step(x, dy, *arrays):
        weights, m, v = (arrays[i : i + 3] for i in (0, 3, 6))
        layers = weights[0].shape[0]
        h, kept = x[0], []
        for number in range(layers):
            kept.append(h)
            h = layer(h, {name: w[number] for name, w in zip(NAMES, weights, strict=True)})
        by_h, summed = dy[0], [None] * layers
        for number in reversed(range(layers)):
            _, back = jax.vjp(lambda w, h: layer(h, w), {name: w[number] for name, w in zip(NAMES, weights, strict=True)}, kept[number])
            by_w, by_h = back(by_h)
            summed[number] = [lax.psum(by_w[name], "dp") for name in NAMES]
        gradients = [jnp.stack([summed[number][i] for number in range(layers)]).astype(jnp.float32) for i in range(3)]
        new = [adamw(w.astype(jnp.float32), m, v, g) for w, m, v, g in zip(weights, m, v, gradients, strict=True)]
        return tuple(one[which] for which in range(3) for one in new)

    return jax.shard_map(
        step,
        mesh=mesh,
        in_specs=(P(("rep", "dp"), None, None),) * 2 + (P(None, None, None),) * 9,
        out_specs=(P("rep", None, None),) * 9,
        check_vma=False,
    )
```

profile of v0, /device:TPU:0, one launch (start us, length us, event | category | flops | bytes accessed | tf_op | source)
XLA Modules:
  0.0 903.0 jit_solution(8025111576543101130)
XLA Ops:
  7.2 0.0 all-reduce.3.cloned.1.call-start
  7.2 6.1 copy.20
  13.3 2.8 fusion.30
  16.1 0.0 slice-start.3
  16.1 6.2 copy.21
  22.4 16.6 %convolution_convert_fusion.1 = bf16[2048,2560]{1,0:T(8,128)(2,1)} fusion(bf16[2,2560,896]{2,1,0:T(8,128)(2,1)} %param.15, bf16[1,2048,896]{2,1,0:T(8,128)(2,1)} %param.12), kind=kOutput, calls=%fused_computation.54 | convolution fusion | flops 9400483840 | bytes 18743296 | tf_op jit(solution)/shard_map/transpose(jvp())/dot_general | solution.py:10
  39.0 0.0 slice-done.4
  39.0 14.2 %fusion.64 = f32[2048,2560]{1,0:T(8,128)} fusion(bf16[2,896,2560]{2,1,0:T(8,128)(2,1)S(1)} %bitcast.77, bf16[1,2048,896]{2,1,0:T(8,128)(2,1)S(1)} %copy-done.2, f32[2048]{0:T(1024)S(1)} %add_rsqrt_fusion), kind=kOutput, calls=%fused_computation.96 | convolution fusion | flops 9400745984 | bytes 29237248 | tf_op jit(solution)/shard_map/dot_general | solution.py:21
  53.2 0.0 copy-done.7
  53.2 26.3 %multiply_convert_fusion.1 = (bf16[2048,2560]{1,0:T(8,128)(2,1)}, f32[2048,2560]{1,0:T(8,128)}) fusion(f32[2048,2560]{1,0:T(8,128)} %fusion.64, bf16[2,896,2560]{2,1,0:T(8,128)(2,1)} %param.14, bf16[1,2048,896]{2,1,0:T(8,128)(2,1)} %param.11, f32[2048]{0:T(1024)S(1)} %add_rsqrt_fusion), kind=kOutput, calls=%fused_computation.29 | convolution fusion | flops 9432203264 | bytes 60694528 | tf_op jit(solution)/shard_map/dot_general | solution.py:22
  79.5 0.0 copy-done
  79.5 14.7 %fusion.34 = (f32[2048]{0:T(1024)S(1)}, bf16[2048,896]{0,1:T(8,128)(2,1)S(1)}) fusion(bf16[2048,2560]{1,0:T(8,128)(2,1)} %get-tuple-element.24, bf16[2,2560,896]{2,1,0:T(8,128)(2,1)} %param.15, bf16[1,2048,896]{1,2,0:T(8,128)(2,1)S(1)} %copy-done), kind=kOutput, calls=%fused_computation.67 | convolution fusion | flops 9404413952 | bytes 22421504 | tf_op jit(solution)/shard_map/dot_general | solution.py:10
  94.2 0.0 copy-start.3
  94.2 0.6 copy-done.5
  94.8 1.2 copy-done.3
  96.1 17.1 %fusion.51 = f32[2048,2560]{1,0:T(8,128)} fusion(bf16[2,896,2560]{2,1,0:T(8,128)(2,1)} %param.14, bf16[2048,896]{0,1:T(8,128)(2,1)S(1)} %get-tuple-element.27, f32[2048]{0:T(1024)S(1)} %fusion.92), kind=kOutput, calls=%fused_computation.83 | convolution fusion | flops 9400745984 | bytes 29237248 | tf_op jit(solution)/shard_map/jvp()/dot_general | solution.py:22
  113.2 31.7 %fusion.2 = (bf16[2048,2560]{1,0:T(8,128)(2,1)}, f32[2048,2560]{1,0:T(8,128)}) fusion(f32[2048,2560]{1,0:T(8,128)} %fusion.51, bf16[2048,2560]{1,0:T(8,128)(2,1)} %convolution_convert_fusion.1, bf16[2,896,2560]{2,1,0:T(8,128)(2,1)} %param.13, bf16[2048,896]{0,1:T(8,128)(2,1)} %copy-done.3, f32[2048]{0:T(1024)S(1)} %fusion.92), kind=kOutput, calls=%fused_computation.20 | convolution fusion | flops 9463660544 | bytes 71180288 | tf_op jit(solution)/shard_map/jvp()/dot_general | solution.py:21
  144.9 18.1 %fusion.27 = bf16[2048,896]{0,1:T(8,128)(2,1)} fusion(bf16[2048,2560]{1,0:T(8,128)(2,1)} %convolution_convert_fusion.1, bf16[2,896,2560]{2,1,0:T(8,128)(2,1)} %param.14, f32[2048,2560]{1,0:T(8,128)} %get-tuple-element.29), kind=kOutput, calls=%fused_computation.48 | convolution fusion | flops 9426698240 | bytes 39714816 | tf_op jit(solution)/shard_map/transpose(jvp())/dot_general | solution.py:22
  163.0 18.9 %fusion.45 = bf16[1,896,2560]{2,1,0:T(8,128)(2,1)} fusion(bf16[2048,2560]{1,0:T(8,128)(2,1)} %convolution_convert_fusion.1, bf16[2048,896]{0,1:T(8,128)(2,1)} %copy-done.3, f32[2048]{0:T(1024)S(1)} %fusion.92, f32[2048,2560]{1,0:T(8,128)} %get-tuple-element.29), kind=kOutput, calls=%fused_computation.79 | convolution fusion | flops 9434497024 | bytes 39723008 | tf_op jit(solution)/shard_map/transpose(jvp())/dot_general | solution.py:22
  182.0 21.3 %fusion.43 = bf16[1,2560,896]{2,1,0:T(8,128)(2,1)} fusion(f32[2048,2560]{1,0:T(8,128)} %fusion.51, bf16[1,2048,896]{2,1,0:T(8,128)(2,1)} %param.12, f32[2048,2560]{1,0:T(8,128)} %get-tuple-element.29), kind=kOutput, calls=%fused_computation.77 | convolution fusion | flops 9428992000 | bytes 50200576 | tf_op jit(solution)/shard_map/transpose(jvp())/dot_general | solution.py:10
  203.3 15.1 %fusion.46 = bf16[1,896,2560]{2,1,0:T(8,128)(2,1)} fusion(bf16[2048,2560]{1,0:T(8,128)(2,1)} %get-tuple-element.28, bf16[2048,896]{0,1:T(8,128)(2,1)} %copy-done.3, f32[2048]{0:T(1024)S(1)} %fusion.92), kind=kOutput, calls=%fused_computation.80 | convolution fusion | flops 9400745984 | bytes 18751488 | tf_op jit(solution)/shard_map/transpose(jvp())/dot_general | solution.py:21
  218.4 17.0 %fusion.36 = (f32[2048]{0:T(1024)S(1)}, bf16[2048,896]{0,1:T(8,128)(2,1)}) fusion(bf16[2048,896]{0,1:T(8,128)(2,1)} %copy-done.3, bf16[2048,896]{0,1:T(8,128)(2,1)} %fusion.27, bf16[2048,2560]{1,0:T(8,128)(2,1)} %get-tuple-element.28, bf16[2,896,2560]{2,1,0:T(8,128)(2,1)} %param.13), kind=kOutput, calls=%fused_computation.69 | convolution fusion | flops 9404413952 | bytes 26091520 | tf_op jit(solution)/shard_map/transpose(jvp())/dot_general | solution.py:21
  235.5 7.6 fusion.76
  243.1 0.0 copy-start.4
  243.1 15.7 %convolution_convert_fusion = bf16[2048,2560]{1,0:T(8,128)(2,1)} fusion(bf16[2048,896]{0,1:T(8,128)(2,1)} %fusion.76, bf16[2,2560,896]{2,1,0:T(8,128)(2,1)S(1)} %bitcast.75), kind=kOutput, calls=%fused_computation.53 | convolution fusion | flops 9400483840 | bytes 18743296 | tf_op jit(solution)/shard_map/transpose(jvp())/dot_general | solution.py:10
  258.8 15.5 %fusion.47 = bf16[1,2560,896]{2,1,0:T(8,128)(2,1)} fusion(bf16[2048,2560]{1,0:T(8,128)(2,1)} %get-tuple-element.24, bf16[2048,896]{0,1:T(8,128)(2,1)S(1)} %copy-done.4), kind=kOutput, calls=%fused_computation.81 | convolution fusion | flops 9397534720 | bytes 18743296 | tf_op jit(solution)/shard_map/transpose(jvp())/dot_general | solution.py:10
  274.3 18.5 %fusion.44 = bf16[1,896,2560]{2,1,0:T(8,128)(2,1)} fusion(bf16[2048,2560]{1,0:T(8,128)(2,1)} %convolution_convert_fusion, f32[2048,2560]{1,0:T(8,128)} %fusion.64, bf16[1,2048,896]{1,2,0:T(8,128)(2,1)} %copy.20, f32[2048]{0:T(1024)S(1)} %copy-done.8), kind=kOutput, calls=%fused_computation.78 | convolution fusion | flops 9434497024 | bytes 39723008 | tf_op jit(solution)/shard_map/transpose(jvp())/dot_general | solution.py:22
  292.8 24.5 %fusion.48 = bf16[1,896,2560]{2,1,0:T(8,128)(2,1)} fusion(f32[2048,2560]{1,0:T(8,128)} %fusion.64, f32[2048,2560]{1,0:T(8,128)} %get-tuple-element.25, bf16[2048,2560]{1,0:T(8,128)(2,1)} %convolution_convert_fusion, bf16[1,2048,896]{1,2,0:T(8,128)(2,1)} %copy.20, f32[2048]{0:T(1024)S(1)} %copy-done.8), kind=kOutput, calls=%fused_computation.82 | convolution fusion | flops 9460711424 | bytes 60694528 | tf_op jit(solution)/shard_map/transpose(jvp())/dot_general | solution.py:21
  317.3 0.0 all-reduce.3.cloned.1.call-update
  317.3 475.8 %all-reduce.3.cloned.1.call-done = (bf16[1,896,2560]{2,1,0:T(8,128)(2,1)}, bf16[1,896,2560]{2,1,0:T(8,128)(2,1)}, bf16[1,896,2560]{2,1,0:T(8,128)(2,1)}, bf16[1,...) async-done(((bf16[1,896,2560]{2,1,0:T(8,128)(2,1)}, bf16[1,896,2560]{2,1,0:T(8,128)(2,1)}, bf16[1,896,2560]{2,1,0:T(8,128)(2,1)}, ...) | async-done | bytes 27525136 | tf_op jit(solution)/shard_map/psum | solution.py:45
  793.1 35.4 %fusion.21 = (bf16[2,2560,896]{2,1,0:T(8,128)(2,1)}, f32[2,2560,896]{2,1,0:T(8,128)}, f32[2,2560,896]{2,1,0:T(8,128)}) fusion(bf16[2,2560,896]{2,1,0:T(8,128)(2,1)} %param.15, bf16[1,2560,896]{2,1,0:T(8,128)(2,1)} %get-tuple-element.13, bf16[1,2560,896]{2,1,0:T(8,128)(2,1)} %get-tuple-element.14, f32[2,2560,896]{2,1,0:T(8,128)} %param.21, ...), kind=kLoop, calls=%fused_computation.42 | loop fusion | flops 87162880 | bytes 100925440 | tf_op jit(solution)/shard_map/convert_element_type | solution.py:30
  828.5 67.2 %fusion.13 = (bf16[2,896,2560]{2,1,0:T(8,128)(2,1)}, f32[2,896,2560]{2,1,0:T(8,128)}, f32[2,896,2560]{2,1,0:T(8,128)}, bf16[2,896,2560]{2,1,0:T(8,128)(2,1)}, f3...) fusion(bf16[2,896,2560]{2,1,0:T(8,128)(2,1)} %param.13, bf16[1,896,2560]{2,1,0:T(8,128)(2,1)} %get-tuple-element.9, ...), kind=kLoop, calls=%fused_computation.34 | loop fusion | flops 174325760 | bytes 201850880 | tf_op jit(solution)/shard_map/convert_element_type | solution.py:30
  (27 shorter events, 0.1 us)
Async XLA Ops:
  7.2 786.0 %all-reduce.3.cloned.1.call-start = ((), (), s32[]{:S(2)}) async-start(), calls=%async_computation | async-start | bytes 55050240 | tf_op jit(solution)/shard_map/psum | solution.py:45
  16.1 37.1 %copy-start.7 = (f32[2048]{0:T(1024)}, f32[2048]{0:T(1024)S(1)}, u32[]{:S(2)}) copy-start(f32[2048]{0:T(1024)S(1)} %add_rsqrt_fusion) | copy-start | bytes 24580
  16.1 22.9 %slice-start.3 = ((s8[9175040]{0:T(1024)(128)(4,1)}), s8[786432]{0:T(1024)(128)(4,1)S(1)}, s32[]{:S(2)}) async-start(s8[9175040]{0:T(1024)(128)(4,1)} %bitcast.76), calls=%async_computation.4 | async-start | bytes 1572864
  22.3 16.6 %slice-start.4 = ((s8[9175040]{0:T(1024)(128)(4,1)}), s8[4194304]{0:T(1024)(128)(4,1)S(1)}, s32[]{:S(2)}) async-start(s8[9175040]{0:T(1024)(128)(4,1)} %bitcast.76), calls=%async_computation.5 | async-start | bytes 8388608
  22.4 16.6 %slice-start.5 = ((s8[9175040]{0:T(1024)(128)(4,1)}), s8[4194304]{0:T(1024)(128)(4,1)S(1)}, s32[]{:S(2)}) async-start(s8[9175040]{0:T(1024)(128)(4,1)} %bitcast.76), calls=%async_computation.6 | async-start | bytes 8388608
  22.4 16.6 %copy-start.2 = (bf16[1,2048,896]{2,1,0:T(8,128)(2,1)S(1)}, bf16[1,2048,896]{2,1,0:T(8,128)(2,1)}, u32[]{:S(2)}) copy-start(bf16[1,2048,896]{2,1,0:T(8,128)(2,1)} %param.11) | copy-start | bytes 11010052
  53.2 26.3 %copy-start = (bf16[1,2048,896]{1,2,0:T(8,128)(2,1)S(1)}, bf16[1,2048,896]{1,2,0:T(8,128)(2,1)}, u32[]{:S(2)}) copy-start(bf16[1,2048,896]{1,2,0:T(8,128)(2,1)} %copy.20) | copy-start | bytes 11010052
  94.2 0.6 copy-start.5
  94.2 1.8 copy-start.3
  203.3 39.8 %slice-start = ((s8[9175040]{0:T(1024)(128)(4,1)}), s8[4194304]{0:T(1024)(128)(4,1)S(1)}, s32[]{:S(2)}) async-start(s8[9175040]{0:T(1024)(128)(4,1)} %bitcast.74), calls=%async_computation.1 | async-start | bytes 8388608
  203.3 39.8 %slice-start.1 = ((s8[9175040]{0:T(1024)(128)(4,1)}), s8[4194304]{0:T(1024)(128)(4,1)S(1)}, s32[]{:S(2)}) async-start(s8[9175040]{0:T(1024)(128)(4,1)} %bitcast.74), calls=%async_computation.2 | async-start | bytes 8388608
  218.4 17.0 %copy-start.6 = (f32[2048]{0:T(1024)S(1)}, f32[2048]{0:T(1024)}, u32[]{:S(2)}) copy-start(f32[2048]{0:T(1024)} %copy-done.5) | copy-start | bytes 24580
  218.4 17.0 %copy-start.1 = (bf16[1,2048,896]{1,2,0:T(8,128)(2,1)S(1)}, bf16[1,2048,896]{1,2,0:T(8,128)(2,1)}, u32[]{:S(2)}) copy-start(bf16[1,2048,896]{1,2,0:T(8,128)(2,1)} %copy.21) | copy-start | bytes 11010052
  218.4 24.7 %slice-start.2 = ((s8[9175040]{0:T(1024)(128)(4,1)}), s8[786432]{0:T(1024)(128)(4,1)S(1)}, s32[]{:S(2)}) async-start(s8[9175040]{0:T(1024)(128)(4,1)} %bitcast.74), calls=%async_computation.3 | async-start | bytes 1572864
  243.1 15.7 %copy-start.4 = (bf16[2048,896]{0,1:T(8,128)(2,1)S(1)}, bf16[2048,896]{0,1:T(8,128)(2,1)}, u32[]{:S(2)}) copy-start(bf16[2048,896]{0,1:T(8,128)(2,1)} %fusion.76) | copy-start | bytes 11010052
  258.8 15.5 %copy-start.8 = (f32[2048]{0:T(1024)S(1)}, f32[2048]{0:T(1024)}, u32[]{:S(2)}) copy-start(f32[2048]{0:T(1024)} %copy-done.7) | copy-start | bytes 24580
Sparse Core Ops, SparseCore 0:
  317.4 475.6 all-reduce.2
where the time goes:
time: 911 us; the launch traced here: 903 us
  waiting for transfers between devices  476 us (52%)
  matrix products  285 us (31%)
  other arithmetic  113 us (12%)
  between operations  14.6 us (2%)
  local copies, waits for them, and re-layouts  14.2 us (2%)
    psum x1, waiting for transfers between devices, step(): summed[number] = [lax.psum(by_w[name], 'dp') for name in NAMES]  476 us
    convert_element_type x2, other arithmetic, adamw(): return ((w - 0.02 * step).astype(jnp.bfloat16), m, v)  103 us
    dot_general x5, matrix products, layer(): gate = jnp.dot(a, w['w_gate'], preferred_element_type=jnp.float32)  103 us
    dot_general x5, matrix products, layer(): up = jnp.dot(a, w['w_up'], preferred_element_type=jnp.float32)  99 us
    dot_general x5, matrix products, matmul(): jnp.dot(a, w, preferred_element_type=jnp.float32).astype(jnp.bfloat16)  83.8 us
  transfers between devices with their start and end apart: 1, of which 1 were waited for; matrix products, arithmetic and copies ran while one was open for 0% of the time, Pallas kernels for 0%

commit v1 on v0

v1 whole, which is shorter than its diff:
```python
import functools

import jax
import jax.numpy as jnp
from jax import lax
from jax.experimental import pallas as pl
from jax.experimental.pallas import tpu as pltpu
from jax.sharding import PartitionSpec as P

MESH = pl.DeviceIdType.MESH
F32, BF16 = jnp.float32, jnp.bfloat16
TOKENS, D, FF = 2048, 896, 2560
BLOCK = 256
PER_LAYER = FF // BLOCK
BLOCKS = 2 * PER_LAYER
TILE = 512
HALF, QUARTER = D // 2, D // 4
LANES = 128
SLOTS_A = {1: 2, 2: 2, 3: 4, 4: 2, 5: 4, 6: 2, 7: 2}
SLOTS_B = {1: 2, 2: 6, 3: 2, 4: 2, 5: 2, 6: 6, 7: 2}


def nt(a, b):
    return lax.dot_general(a, b, (((1,), (1,)), ((), ())), preferred_element_type=F32)


def nn(a, b):
    return jnp.dot(a, b, preferred_element_type=F32)


def rows(start, size):
    return pl.ds(pl.multiple_of(start, 32), size)


def scale_of(wide):
    return lax.rsqrt(jnp.mean(wide * wide, -1, keepdims=True) + 1e-6)


def step_kernel(x_hbm, dy_hbm, wg_hbm, wu_hbm, wd_hbm, ga, gb, P_, H, DY, AT, DT, ACC, HID, DG, DU, wg_v, wu_v, wd_v, *comm):
    (sb_a, keep_a, r1_a, s2_a, k2_a, r2_a, s3_a, acc_a, r3_a, s4_a, r4_a, g_a,
     sb_b, keep_b, r1_b, s2_b, acc1_b, r2_b, s3_b, k2_b, r3_b, s4_b, r4_b, g_b,
     load_sem, w_sem, loc_a, loc_b, send_a, send_b, *recvs) = comm
    recv_a = dict(zip(range(1, 8), recvs[:7], strict=True))
    recv_b = dict(zip(range(1, 8), recvs[7:], strict=True))
    me = lax.axis_index("dp")
    c = me % 2
    z = (me // 2) % 4
    y = me // 8
    odd = z % 2
    high = z // 2
    inner = (odd + high) == 1
    end = (odd + high) != 1
    to_core = me + 1 - 2 * c
    to_y = me + 8 - 16 * y
    to_z = me + 2 - 4 * odd
    to_mid = me + 2 - 4 * high

    def remote(src, dst, send, recv, to):
        return pltpu.make_async_remote_copy(
            src_ref=src, dst_ref=dst, send_sem=send, recv_sem=recv, device_id={"dp": to}, device_id_type=MESH
        )

    barrier = pltpu.get_barrier_semaphore()
    for to in (to_core, to_y, to_z):
        pl.semaphore_signal(barrier, inc=1, device_id={"dp": to}, device_id_type=MESH)

    @pl.when(inner)
    def _():
        pl.semaphore_signal(barrier, inc=1, device_id={"dp": to_mid}, device_id_type=MESH)
        pl.semaphore_wait(barrier, 4)

    @pl.when(end)
    def _():
        pl.semaphore_wait(barrier, 3)

    def weight_copies(i):
        layer, j, slot = (i // PER_LAYER) % 2, i % PER_LAYER, i % 2
        cols = pl.ds(pl.multiple_of(j * BLOCK, BLOCK), BLOCK)
        return (
            pltpu.make_async_copy(wg_hbm.at[layer, :, cols], wg_v.at[slot], w_sem.at[slot, 0]),
            pltpu.make_async_copy(wu_hbm.at[layer, :, cols], wu_v.at[slot], w_sem.at[slot, 1]),
            pltpu.make_async_copy(wd_hbm.at[layer, cols, :], wd_v.at[slot], w_sem.at[slot, 2]),
        )

    def fetch(i):
        for copy in weight_copies(i):
            copy.start()

    def arrive(i):
        for copy in weight_copies(i):
            copy.wait()

    fetch(0)
    load_x = pltpu.make_async_copy(x_hbm.at[0], H, load_sem.at[0])
    load_dy = pltpu.make_async_copy(dy_hbm.at[0], DY, load_sem.at[1])
    load_x.start()
    load_dy.start()
    load_x.wait()

    def tiles(body, tile=TILE):
        def one(k, carry):
            body(pl.ds(pl.multiple_of(k * tile, tile), tile))
            return carry

        lax.fori_loop(0, TOKENS // tile, one, 0)

    def norm_into(source):
        def body(at):
            wide = source[at, :].astype(F32)
            P_[at, :] = (wide * scale_of(wide)).astype(BF16)
            ACC[at, :] = jnp.zeros((128, D), F32)

        tiles(body, 128)

    def flip(source, target):
        def body(at):
            target[:, at] = source[at, :].T

        tiles(body, 256)

    norm_into(H)

    def forward(i, carry):
        slot = i % 2
        arrive(i)
        fetch(i + 1)

        def body(at):
            a = P_[at, :]
            gate, up = nn(a, wg_v[slot]), nn(a, wu_v[slot])
            hid = (gate * jax.nn.sigmoid(gate) * up).astype(BF16)
            ACC[at, :] += nn(hid, wd_v[slot])

        tiles(body)
        return carry

    lax.fori_loop(0, PER_LAYER, forward, 0)

    def join(at):
        h = (H[at, :].astype(F32) + ACC[at, :].astype(BF16).astype(F32)).astype(BF16)
        H[at, :] = h

    tiles(join, 128)
    norm_into(H)
    load_dy.wait()
    flip(P_, AT)
    flip(DY, DT)

    def own_a(b):
        return ga.at[b, :, rows(c * HALF + y * QUARTER, QUARTER), :]

    def other_a(b):
        return ga.at[b, :, rows(c * HALF + (1 - y) * QUARTER, QUARTER), :]

    def core_of(g, b, which):
        return g.at[b, :, rows(which * HALF, HALF), :]

    def own_b(b):
        return gb.at[b, :, rows(c * HALF + high * QUARTER, QUARTER), :]

    def other_b(b):
        return gb.at[b, :, rows(c * HALF + (1 - high) * QUARTER, QUARTER), :]

    def live(t, s):
        return (t - s >= 0) & (t - s < BLOCKS)

    def a_copy(s, b, src, dst, to):
        return remote(src, dst, send_a.at[s], recv_a[s].at[b % SLOTS_A[s]], to)

    def b_copy(s, b, src, dst, to):
        return remote(src, dst, send_b.at[s], recv_b[s].at[b % SLOTS_B[s]], to)

    def tick_a(t):
        @pl.when(live(t, 7))
        def _():
            b = t - 7
            a_copy(7, b, core_of(ga, b, c), core_of(ga, b, c), to_core).wait_send()
            a_copy(7, b, core_of(ga, b, 1 - c), core_of(ga, b, 1 - c), to_core).wait_recv()

        @pl.when(live(t, 6))
        def _():
            b = t - 6
            a_copy(6, b, own_a(b), own_a(b), to_y).wait_send()
            a_copy(6, b, other_a(b), other_a(b), to_y).wait_recv()
            a_copy(7, b, core_of(ga, b, c), core_of(ga, b, c), to_core).start()

        @pl.when(live(t, 5))
        def _():
            b = t - 5

            @pl.when(inner)
            def _():
                a_copy(5, b, g_a, own_a(b), to_z).wait_send()
                pltpu.make_async_copy(g_a, own_a(b), loc_a).wait()

            @pl.when(end)
            def _():
                a_copy(5, b, g_a, own_a(b), to_z).wait_recv()

            a_copy(6, b, own_a(b), own_a(b), to_y).start()

        @pl.when(live(t, 4) & inner)
        def _():
            b = t - 4
            copy = a_copy(4, b, s4_a, r4_a.at[b % 2], to_mid)
            copy.wait_send()
            copy.wait_recv()
            g_a[...] = (s4_a[...].astype(F32) + r4_a[b % 2].astype(F32)).astype(BF16)
            pltpu.make_async_copy(g_a, own_a(b), loc_a).start()
            a_copy(5, b, g_a, own_a(b), to_z).start()

        @pl.when(live(t, 3))
        def _():
            b = t - 3
            slot = b % SLOTS_A[3]
            copy = a_copy(3, b, s3_a, r3_a.at[slot], to_z)

            @pl.when(end)
            def _():
                copy.wait_send()

            @pl.when(inner)
            def _():
                copy.wait_recv()
                s4_a[...] = (acc_a[...] + r3_a[slot].astype(F32)).astype(BF16)
                a_copy(4, b, s4_a, r4_a.at[b % 2], to_mid).start()

        @pl.when(live(t, 2))
        def _():
            b = t - 2
            copy = a_copy(2, b, s2_a, r2_a.at[b % 2], to_y)
            copy.wait_send()
            copy.wait_recv()
            total = k2_a[...] + r2_a[b % 2].astype(F32)

            @pl.when(inner)
            def _():
                acc_a[...] = total

            @pl.when(end)
            def _():
                s3_a[...] = total.astype(BF16)
                a_copy(3, b, s3_a, r3_a.at[b % SLOTS_A[3]], to_z).start()

        @pl.when(live(t, 1))
        def _():
            b = t - 1
            slot = b % 2
            copy = a_copy(1, b, sb_a.at[slot], r1_a.at[slot], to_core)
            copy.wait_send()
            copy.wait_recv()
            mine, theirs = rows(y * QUARTER, QUARTER), rows((1 - y) * QUARTER, QUARTER)
            k2_a[...] = keep_a[slot, :, mine, :] + r1_a[slot, :, mine, :].astype(F32)
            s2_a[...] = (keep_a[slot, :, theirs, :] + r1_a[slot, :, theirs, :].astype(F32)).astype(BF16)
            a_copy(2, b, s2_a, r2_a.at[slot], to_y).start()

        @pl.when(live(t, 0))
        def _():
            a_copy(1, t, sb_a.at[t % 2], r1_a.at[t % 2], to_core).start()

    def tick_b(t):
        @pl.when(live(t, 7))
        def _():
            b = t - 7
            b_copy(7, b, core_of(gb, b, c), core_of(gb, b, c), to_core).wait_send()
            b_copy(7, b, core_of(gb, b, 1 - c), core_of(gb, b, 1 - c), to_core).wait_recv()

        @pl.when(live(t, 6))
        def _():
            b = t - 6
            copy = b_copy(6, b, core_of(gb, b, c), core_of(gb, b, c), to_z)

            @pl.when(inner)
            def _():
                copy.wait_send()

            @pl.when(end)
            def _():
                copy.wait_recv()

            b_copy(7, b, core_of(gb, b, c), core_of(gb, b, c), to_core).start()

        @pl.when(live(t, 5) & inner)
        def _():
            b = t - 5
            b_copy(5, b, g_b, own_b(b), to_mid).wait_send()
            b_copy(5, b, g_b, other_b(b), to_mid).wait_recv()
            pltpu.make_async_copy(g_b, own_b(b), loc_b).wait()
            b_copy(6, b, core_of(gb, b, c), core_of(gb, b, c), to_z).start()

        @pl.when(live(t, 4) & inner)
        def _():
            b = t - 4
            copy = b_copy(4, b, s4_b, r4_b.at[b % 2], to_y)
            copy.wait_send()
            copy.wait_recv()
            g_b[...] = (s4_b[...].astype(F32) + r4_b[b % 2].astype(F32)).astype(BF16)
            pltpu.make_async_copy(g_b, own_b(b), loc_b).start()
            b_copy(5, b, g_b, own_b(b), to_mid).start()

        @pl.when(live(t, 3) & inner)
        def _():
            b = t - 3
            copy = b_copy(3, b, s3_b, r3_b.at[b % 2], to_mid)
            copy.wait_send()
            copy.wait_recv()
            s4_b[...] = (k2_b[...] + r3_b[b % 2].astype(F32)).astype(BF16)
            b_copy(4, b, s4_b, r4_b.at[b % 2], to_y).start()

        @pl.when(live(t, 2))
        def _():
            b = t - 2
            slot = b % SLOTS_B[2]
            copy = b_copy(2, b, s2_b, r2_b.at[slot], to_z)

            @pl.when(end)
            def _():
                copy.wait_send()

            @pl.when(inner)
            def _():
                copy.wait_recv()
                mine, theirs = rows(high * QUARTER, QUARTER), rows((1 - high) * QUARTER, QUARTER)
                k2_b[...] = acc1_b[:, mine, :] + r2_b[slot, :, mine, :].astype(F32)
                s3_b[...] = (acc1_b[:, theirs, :] + r2_b[slot, :, theirs, :].astype(F32)).astype(BF16)
                b_copy(3, b, s3_b, r3_b.at[b % 2], to_mid).start()

        @pl.when(live(t, 1))
        def _():
            b = t - 1
            slot = b % 2
            copy = b_copy(1, b, sb_b.at[slot], r1_b.at[slot], to_core)
            copy.wait_send()
            copy.wait_recv()
            total = keep_b[slot] + r1_b[slot].astype(F32)

            @pl.when(inner)
            def _():
                acc1_b[...] = total

            @pl.when(end)
            def _():
                s2_b[...] = total.astype(BF16)
                b_copy(2, b, s2_b, r2_b.at[b % SLOTS_B[2]], to_z).start()

        @pl.when(live(t, 0))
        def _():
            b_copy(1, t, sb_b.at[t % 2], r1_b.at[t % 2], to_core).start()

    def turn():
        load = pltpu.make_async_copy(x_hbm.at[0], P_, load_sem.at[0])
        load.start()

        def body(at):
            wide = H[at, :].astype(F32)
            scale = scale_of(wide)
            da = ACC[at, :].astype(BF16).astype(F32)
            along = jnp.sum(da * wide, -1, keepdims=True) * (scale * scale * scale) * (1.0 / D)
            by_h = (da * scale - wide * along).astype(BF16).astype(F32)
            DY[at, :] = (DY[at, :].astype(F32) + by_h).astype(BF16)

        tiles(body, 128)
        flip(DY, DT)
        load.wait()
        norm_into(P_)
        flip(P_, AT)

    def gradients(t):
        slot = (t + PER_LAYER) % 2

        def body(at):
            a = P_[at, :]
            gate, up = nn(a, wg_v[slot]), nn(a, wu_v[slot])
            by_hid = nt(DY[at, :], wd_v[slot]).astype(BF16).astype(F32)
            sig = jax.nn.sigmoid(gate)
            act = gate * sig
            HID[at, :] = (act * up).astype(BF16)
            by_gate = (by_hid * up * (sig + act * (1.0 - sig))).astype(BF16)
            by_up = (by_hid * act).astype(BF16)
            DG[at, :] = by_gate
            DU[at, :] = by_up

        tiles(body)

        @pl.when(t < PER_LAYER)
        def _():
            def body(at):
                ACC[at, :] += nt(DG[at, :], wg_v[slot]) + nt(DU[at, :], wu_v[slot])

            tiles(body)

    def weights_of(t):
        slot = t % 2
        for m, (left, right) in enumerate(((AT, DG), (AT, DU), (DT, HID))):
            total = nn(left[rows((1 - c) * HALF, HALF), :], right[...]).astype(BF16)
            sb_a[slot, m] = total[:, :LANES]
            sb_b[slot, m] = total[:, LANES:]
            total = nn(left[rows(c * HALF, HALF), :], right[...])
            keep_a[slot, m] = total[:, :LANES]
            keep_b[slot, m] = total[:, LANES:]

    def main(t, carry):
        @pl.when(t == PER_LAYER)
        def _():
            turn()

        @pl.when(t < BLOCKS)
        def _():
            arrive(t + PER_LAYER)

            @pl.when(t < BLOCKS - 1)
            def _():
                fetch(t + PER_LAYER + 1)

            gradients(t)

        tick_b(t - 1)

        @pl.when(t < BLOCKS)
        def _():
            weights_of(t)

        tick_a(t)
        return carry

    lax.fori_loop(0, BLOCKS + 8, main, 0)


def summed_gradients(x, dy, wg, wu, wd):
    unit = lambda n, height, dtype: pltpu.VMEM((n, 3, height, LANES) if n else (3, height, LANES), dtype)
    scratch = [
        pltpu.VMEM((TOKENS, D), BF16),
        pltpu.VMEM((TOKENS, D), BF16),
        pltpu.VMEM((TOKENS, D), BF16),
        pltpu.VMEM((D, TOKENS), BF16),
        pltpu.VMEM((D, TOKENS), BF16),
        pltpu.VMEM((TOKENS, D), F32),
        pltpu.VMEM((TOKENS, BLOCK), BF16),
        pltpu.VMEM((TOKENS, BLOCK), BF16),
        pltpu.VMEM((TOKENS, BLOCK), BF16),
        pltpu.VMEM((2, D, BLOCK), BF16),
        pltpu.VMEM((2, D, BLOCK), BF16),
        pltpu.VMEM((2, BLOCK, D), BF16),
        unit(2, HALF, BF16), unit(2, HALF, F32), unit(2, HALF, BF16),
        unit(0, QUARTER, BF16), unit(0, QUARTER, F32), unit(2, QUARTER, BF16),
        unit(0, QUARTER, BF16), unit(0, QUARTER, F32), unit(SLOTS_A[3], QUARTER, BF16),
        unit(0, QUARTER, BF16), unit(2, QUARTER, BF16), unit(0, QUARTER, BF16),
        unit(2, HALF, BF16), unit(2, HALF, F32), unit(2, HALF, BF16),
        unit(0, HALF, BF16), unit(0, HALF, F32), unit(SLOTS_B[2], HALF, BF16),
        unit(0, QUARTER, BF16), unit(0, QUARTER, F32), unit(2, QUARTER, BF16),
        unit(0, QUARTER, BF16), unit(2, QUARTER, BF16), unit(0, QUARTER, BF16),
        pltpu.SemaphoreType.DMA((2,)),
        pltpu.SemaphoreType.DMA((2, 3)),
        pltpu.SemaphoreType.DMA,
        pltpu.SemaphoreType.DMA,
        pltpu.SemaphoreType.DMA((8,)),
        pltpu.SemaphoreType.DMA((8,)),
        *[pltpu.SemaphoreType.DMA((SLOTS_A[s],)) for s in range(1, 8)],
        *[pltpu.SemaphoreType.DMA((SLOTS_B[s],)) for s in range(1, 8)],
    ]
    out = jax.ShapeDtypeStruct((BLOCKS, 3, D, LANES), BF16)
    return pl.pallas_call(
        step_kernel,
        out_shape=(out, out),
        in_specs=[pl.BlockSpec(memory_space=pl.ANY)] * 5,
        out_specs=(pl.BlockSpec(memory_space=pl.ANY),) * 2,
        scratch_shapes=scratch,
        compiler_params=pltpu.CompilerParams(collective_id=0, has_side_effects=True, vmem_limit_bytes=62 * 2**20),
        name="gradients",
    )(x, dy, wg, wu, wd)


def adamw(w, m, v, g):
    m = 0.9 * m + 0.1 * g
    v = 0.95 * v + 0.05 * g * g
    step = m * lax.rsqrt(v + 1e-8) + 0.1 * w
    return (w - 0.02 * step).astype(BF16), m, v


def update_wide(w_ref, m_ref, v_ref, ga_ref, gb_ref, w_out, m_out, v_out):
    for j in range(FF // LANES):
        at = slice(j * LANES, (j + 1) * LANES)
        g = (ga_ref, gb_ref)[j % 2][j // 2, 0].astype(F32)
        w_out[0, :, at], m_out[0, :, at], v_out[0, :, at] = adamw(
            w_ref[0, :, at].astype(F32), m_ref[0, :, at], v_ref[0, :, at], g
        )


def update_tall(w_ref, m_ref, v_ref, ga_ref, gb_ref, w_out, m_out, v_out):
    for k, g_ref in enumerate((ga_ref, gb_ref)):
        at = slice(k * LANES, (k + 1) * LANES)
        g = g_ref[0, 0].T.astype(F32)
        w_out[0, at], m_out[0, at], v_out[0, at] = adamw(w_ref[0, at].astype(F32), m_ref[0, at], v_ref[0, at], g)


def update(which, w, m, v, ga, gb):
    if which < 2:
        height = 112
        kernel, grid = update_wide, (2, D // height)
        spec = pl.BlockSpec((1, height, FF), lambda l, i: (l, i, 0))
        g_spec = pl.BlockSpec((PER_LAYER, 1, height, LANES), lambda l, i: (1 - l, which, i, 0))
    else:
        kernel, grid = update_tall, (2, PER_LAYER)
        spec = pl.BlockSpec((1, BLOCK, D), lambda l, i: (l, i, 0))
        g_spec = pl.BlockSpec((1, 1, D, LANES), lambda l, i: ((1 - l) * PER_LAYER + i, which, 0, 0))
    return pl.pallas_call(
        kernel,
        grid=grid,
        in_specs=[spec] * 3 + [g_spec] * 2,
        out_specs=[spec] * 3,
        out_shape=[jax.ShapeDtypeStruct(w.shape, t) for t in (BF16, F32, F32)],
        compiler_params=pltpu.CompilerParams(vmem_limit_bytes=48 * 2**20),
        name=f"update_{which}",
    )(w, m, v, ga, gb)


def solution(mesh):
    def step(x, dy, *arrays):
        weights, m, v = (arrays[i : i + 3] for i in (0, 3, 6))
        ga, gb = summed_gradients(x, dy, *weights)
        new = [update(i, weights[i], m[i], v[i], ga, gb) for i in range(3)]
        return tuple(one[which] for which in range(3) for one in new)

    return jax.shard_map(
        step,
        mesh=mesh,
        in_specs=(P(("rep", "dp"), None, None),) * 2 + (P(None, None, None),) * 9,
        out_specs=(P("rep", None, None),) * 9,
        check_vma=False,
    )
```

time: 911 us -> 461 us (0.51)
  waiting for transfers between devices: 476 us -> 0 us
  Pallas kernels: 0 us -> 460 us
  matrix products: 285 us -> 0 us
  other arithmetic: 113 us -> 0 us
  local copies, waits for them, and re-layouts: 14.2 us -> 0 us
  between operations: 14.6 us -> 0.65 us
    psum x1 -> x0, waiting for transfers between devices: 476 us -> none  [step(): summed[number] = [lax.psum(by_w[name], 'dp') for name in NAMES]]
    pallas_call x0 -> x4, Pallas kernels: none -> 460 us  [the longest x1 347 us: summed_gradients(): pl.pallas_call(step_kernel, out_shape=(out, out), in_specs=[pl.BlockSpec(...]
    dot_general x15 -> x0, matrix products: 285 us -> none  [the longest x5 103 us: layer(): gate = jnp.dot(a, w['w_gate'], preferred_element_type=jnp.float32)]
    convert_element_type x2 -> x0, other arithmetic: 103 us -> none  [adamw(): return ((w - 0.02 * step).astype(jnp.bfloat16), m, v)]
    unnamed x32 -> x0, local copies, waits for them, and re-layouts: 14.2 us -> none
  transfers between devices with their start and end apart: 1 -> 0, of which waited for: 1 -> 0; matrix products, arithmetic and copies ran while one was open for 0% -> 0% of each run, Pallas kernels for 0% -> 0%
where the time goes in v1:
time: 461 us
  Pallas kernels  460 us (100%)
    pallas_call x1, Pallas kernels, summed_gradients(): pl.pallas_call(step_kernel, out_shape=(out, out), in_specs=[pl.BlockSpec(...  347 us
    pallas_call x3, Pallas kernels, update(): pl.pallas_call(kernel, grid=grid, in_specs=[spec] * 3 + [g_spec] * 2, out...  113 us

profile of v1, /device:TPU:0, one launch (start us, length us, event | category | flops | bytes accessed | tf_op | source)
XLA Modules:
  0.0 460.8 jit_solution(552635655787049190)
XLA Ops:
  0.6 346.9 %gradients.1 = (bf16[20,3,896,128]{3,2,1,0:T(8,128)(2,1)}, bf16[20,3,896,128]{3,2,1,0:T(8,128)(2,1)}) custom-call(bf16[1,2048,896]{2,1,0:T(8,128)(2,1)} %x_hbm.1, bf16[1,2048,896]{2,1,0:T(8,128)(2,1)} %dy_hbm.1, bf16[2,896,2560]{2,1,0:T(8,128)(2,1)} %w_ref.3, bf16[2,896,2560]{2,1,0:T(8,128)(2,1)} %w_ref.4, bf16[2,2560,896]{2,1,0:T(8,128)(2,1)} %w_ref.5), custom_call_target="tpu_custom_call" | custom-call | tf_op jit(solution)/shard_map/gradients/pallas_call | solution.py:462
  347.5 40.3 %update_2.1 = (bf16[2,2560,896]{2,1,0:T(8,128)(2,1)}, f32[2,2560,896]{2,1,0:T(8,128)}, f32[2,2560,896]{2,1,0:T(8,128)}) custom-call(bf16[2,2560,896]{2,1,0:T(8,128)(2,1)} %w_ref.5, f32[2,2560,896]{2,1,0:T(8,128)} %m_ref.5, f32[2,2560,896]{2,1,0:T(8,128)} %v_ref.5, bf16[20,3,896,128]{3,2,1,0:T(8,128)(2,1)} %get-tuple-element.20.ga_ref, ...), custom_call_target="tpu_custom_call" | custom-call | tf_op jit(solution)/shard_map/update_2/pallas_call | solution.py:506
  387.9 36.5 %update_1.1 = (bf16[2,896,2560]{2,1,0:T(8,128)(2,1)}, f32[2,896,2560]{2,1,0:T(8,128)}, f32[2,896,2560]{2,1,0:T(8,128)}) custom-call(bf16[2,896,2560]{2,1,0:T(8,128)(2,1)} %w_ref.4, f32[2,896,2560]{2,1,0:T(8,128)} %m_ref.4, f32[2,896,2560]{2,1,0:T(8,128)} %v_ref.4, bf16[20,3,896,128]{3,2,1,0:T(8,128)(2,1)} %get-tuple-element.20.ga_ref, ...), custom_call_target="tpu_custom_call" | custom-call | tf_op jit(solution)/shard_map/update_1/pallas_call | solution.py:506
  424.4 36.5 %update_0.1 = (bf16[2,896,2560]{2,1,0:T(8,128)(2,1)}, f32[2,896,2560]{2,1,0:T(8,128)}, f32[2,896,2560]{2,1,0:T(8,128)}) custom-call(bf16[2,896,2560]{2,1,0:T(8,128)(2,1)} %w_ref.3, f32[2,896,2560]{2,1,0:T(8,128)} %m_ref.3, f32[2,896,2560]{2,1,0:T(8,128)} %v_ref.3, bf16[20,3,896,128]{3,2,1,0:T(8,128)(2,1)} %get-tuple-element.20.ga_ref, ...), custom_call_target="tpu_custom_call" | custom-call | tf_op jit(solution)/shard_map/update_0/pallas_call | solution.py:506

commit v2 on v1

v2 whole, which is shorter than its diff:
```python
import jax
import jax.numpy as jnp
from jax import lax
from jax.experimental import pallas as pl
from jax.experimental.pallas import tpu as pltpu
from jax.sharding import PartitionSpec as P

MESH = pl.DeviceIdType.MESH
F32, BF16 = jnp.float32, jnp.bfloat16
TOKENS, D, FF = 2048, 896, 2560
BLOCK = 256
PER_LAYER = FF // BLOCK
BLOCKS = 2 * PER_LAYER
TILE = 512
HALF, QUARTER = D // 2, D // 4
LANES = 128
SLOTS_A = {2: 2, 3: 4, 4: 2, 5: 4, 6: 2, 7: 2}
SLOTS_B = {2: 6, 3: 2, 4: 2, 5: 2, 6: 6, 7: 2}


def nt(a, b):
    return lax.dot_general(a, b, (((1,), (1,)), ((), ())), preferred_element_type=F32)


def nn(a, b):
    return jnp.dot(a, b, preferred_element_type=F32)


def rows(start, size):
    return pl.ds(pl.multiple_of(start, 32), size)


def scale_of(wide):
    return lax.rsqrt(jnp.mean(wide * wide, -1, keepdims=True) + 1e-6)


def step_kernel(x_hbm, dy_hbm, wg_hbm, wu_hbm, wd_hbm, ga, gb, P_, H, DY, AT, DT, ACC, HID, DG, DU, wg_v, wu_v, wd_v, *comm):
    (sb_a, keep_a, r1_a, s2_a, k2_a, r2_a, s3_a, acc_a, r3_a, s4_a, r4_a, g_a,
     sb_b, keep_b, r1_b, s2_b, acc1_b, r2_b, s3_b, k2_b, r3_b, s4_b, r4_b, g_b,
     load_sem, w_sem, loc_a, loc_b, first_send, first_recv, send_a, send_b, *recvs) = comm
    recv_a = dict(zip(range(2, 8), recvs[:6], strict=True))
    recv_b = dict(zip(range(2, 8), recvs[6:], strict=True))
    me = lax.axis_index("dp")
    c = me % 2
    z = (me // 2) % 4
    y = me // 8
    odd = z % 2
    high = z // 2
    inner = (odd + high) == 1
    end = (odd + high) != 1
    to_core = me + 1 - 2 * c
    to_y = me + 8 - 16 * y
    to_z = me + 2 - 4 * odd
    to_mid = me + 2 - 4 * high

    def remote(src, dst, send, recv, to):
        return pltpu.make_async_remote_copy(
            src_ref=src, dst_ref=dst, send_sem=send, recv_sem=recv, device_id={"dp": to}, device_id_type=MESH
        )

    barrier = pltpu.get_barrier_semaphore()
    for to in (to_core, to_y, to_z):
        pl.semaphore_signal(barrier, inc=1, device_id={"dp": to}, device_id_type=MESH)

    @pl.when(inner)
    def _():
        pl.semaphore_signal(barrier, inc=1, device_id={"dp": to_mid}, device_id_type=MESH)
        pl.semaphore_wait(barrier, 4)

    @pl.when(end)
    def _():
        pl.semaphore_wait(barrier, 3)

    def weight_copies(i):
        layer, j, slot = (i // PER_LAYER) % 2, i % PER_LAYER, i % 2
        cols = pl.ds(pl.multiple_of(j * BLOCK, BLOCK), BLOCK)
        return (
            pltpu.make_async_copy(wg_hbm.at[layer, :, cols], wg_v.at[slot], w_sem.at[slot, 0]),
            pltpu.make_async_copy(wu_hbm.at[layer, :, cols], wu_v.at[slot], w_sem.at[slot, 1]),
            pltpu.make_async_copy(wd_hbm.at[layer, cols, :], wd_v.at[slot], w_sem.at[slot, 2]),
        )

    def fetch(i):
        for copy in weight_copies(i):
            copy.start()

    def arrive(i):
        for copy in weight_copies(i):
            copy.wait()

    fetch(0)
    loads = [
        pltpu.make_async_copy(x_hbm.at[0, k * TILE : (k + 1) * TILE], H.at[k * TILE : (k + 1) * TILE], load_sem.at[k])
        for k in range(TOKENS // TILE)
    ]
    load_dy = pltpu.make_async_copy(dy_hbm.at[0], DY, load_sem.at[TOKENS // TILE])
    for load in loads:
        load.start()
    load_dy.start()

    def tiles(body):
        for k in range(TOKENS // TILE):
            body(slice(k * TILE, (k + 1) * TILE))

    def normed(h):
        wide = h.astype(F32)
        return (wide * scale_of(wide)).astype(BF16)

    def down_of(a, slot):
        gate, up = nn(a, wg_v[slot]), nn(a, wu_v[slot])
        return nn((gate * jax.nn.sigmoid(gate) * up).astype(BF16), wd_v[slot])

    def flip_a_share(i):
        for k in range(TOKENS // TILE):
            q = pl.ds(pl.multiple_of((i * (TOKENS // TILE) + k) * LANES, LANES), LANES)
            AT[0, :, q] = P_[0, q, :].T
            DT[:, q] = DY[q, :].T

    def first(at):
        a = normed(H[at, :])
        P_[0, at, :] = a
        ACC[at, :] = down_of(a, 0)

    def last(at):
        total = ACC[at, :] + down_of(P_[0, at, :], (PER_LAYER - 1) % 2)
        h = (H[at, :].astype(F32) + total.astype(BF16).astype(F32)).astype(BF16)
        H[at, :] = h
        a = normed(h)
        P_[1, at, :] = a
        AT[1, :, at] = a.T
        ACC[at, :] = jnp.zeros((TILE, D), F32)

    def forward(i, flips):
        slot = i % 2
        arrive(i)
        fetch(i + 1)

        def body(at):
            ACC[at, :] += down_of(P_[0, at, :], slot)

        tiles(body)
        if flips:
            flip_a_share(i - 1)

    arrive(0)
    fetch(1)
    for k, load in enumerate(loads):
        load.wait()
        first(slice(k * TILE, (k + 1) * TILE))
    load_dy.wait()
    with_flips = 1 + TILE // LANES

    @pl.loop(1, with_flips)
    def _(i):
        forward(i, True)

    @pl.loop(with_flips, PER_LAYER - 1)
    def _(i):
        forward(i, False)

    arrive(PER_LAYER - 1)
    fetch(PER_LAYER)
    tiles(last)

    def own_a(b):
        return ga.at[b, :, rows(c * HALF + y * QUARTER, QUARTER), :]

    def other_a(b):
        return ga.at[b, :, rows(c * HALF + (1 - y) * QUARTER, QUARTER), :]

    def core_of(g, b, which):
        return g.at[b, :, rows(which * HALF, HALF), :]

    def own_b(b):
        return gb.at[b, :, rows(c * HALF + high * QUARTER, QUARTER), :]

    def other_b(b):
        return gb.at[b, :, rows(c * HALF + (1 - high) * QUARTER, QUARTER), :]

    def live(t, s):
        return (t - s >= 0) & (t - s < BLOCKS)

    def a_copy(s, b, src, dst, to):
        return remote(src, dst, send_a.at[s], recv_a[s].at[b % SLOTS_A[s]], to)

    def b_copy(s, b, src, dst, to):
        return remote(src, dst, send_b.at[s], recv_b[s].at[b % SLOTS_B[s]], to)

    def first_a(b, m):
        slot = b % 2
        return remote(sb_a.at[slot, m], r1_a.at[slot, m], first_send.at[0, slot, m], first_recv.at[0, slot, m], to_core)

    def first_b(b, m):
        slot = b % 2
        return remote(sb_b.at[slot, m], r1_b.at[slot, m], first_send.at[1, slot, m], first_recv.at[1, slot, m], to_core)

    def tick_a(t):
        @pl.when(live(t, 6))
        def _():
            b = t - 6
            a_copy(7, b, core_of(ga, b, c), core_of(ga, b, c), to_core).wait_send()
            a_copy(7, b, core_of(ga, b, 1 - c), core_of(ga, b, 1 - c), to_core).wait_recv()

        @pl.when(live(t, 5))
        def _():
            b = t - 5
            a_copy(6, b, own_a(b), own_a(b), to_y).wait_send()
            a_copy(6, b, other_a(b), other_a(b), to_y).wait_recv()
            a_copy(7, b, core_of(ga, b, c), core_of(ga, b, c), to_core).start()

        @pl.when(live(t, 4))
        def _():
            b = t - 4

            @pl.when(inner)
            def _():
                a_copy(5, b, g_a, own_a(b), to_z).wait_send()
                pltpu.make_async_copy(g_a, own_a(b), loc_a).wait()

            @pl.when(end)
            def _():
                a_copy(5, b, g_a, own_a(b), to_z).wait_recv()

            a_copy(6, b, own_a(b), own_a(b), to_y).start()

        @pl.when(live(t, 3) & inner)
        def _():
            b = t - 3
            copy = a_copy(4, b, s4_a, r4_a.at[b % 2], to_mid)
            copy.wait_send()
            copy.wait_recv()
            g_a[...] = (s4_a[...].astype(F32) + r4_a[b % 2].astype(F32)).astype(BF16)
            pltpu.make_async_copy(g_a, own_a(b), loc_a).start()
            a_copy(5, b, g_a, own_a(b), to_z).start()

        @pl.when(live(t, 2))
        def _():
            b = t - 2
            slot = b % SLOTS_A[3]
            copy = a_copy(3, b, s3_a, r3_a.at[slot], to_z)

            @pl.when(end)
            def _():
                copy.wait_send()

            @pl.when(inner)
            def _():
                copy.wait_recv()
                s4_a[...] = (acc_a[...] + r3_a[slot].astype(F32)).astype(BF16)
                a_copy(4, b, s4_a, r4_a.at[b % 2], to_mid).start()

        @pl.when(live(t, 1))
        def _():
            b = t - 1
            copy = a_copy(2, b, s2_a, r2_a.at[b % 2], to_y)
            copy.wait_send()
            copy.wait_recv()
            total = k2_a[...] + r2_a[b % 2].astype(F32)

            @pl.when(inner)
            def _():
                acc_a[...] = total

            @pl.when(end)
            def _():
                s3_a[...] = total.astype(BF16)
                a_copy(3, b, s3_a, r3_a.at[b % SLOTS_A[3]], to_z).start()

        @pl.when(live(t, 0))
        def _():
            b = t
            slot = b % 2
            for m in range(3):
                first_a(b, m).wait()
            mine, theirs = rows(y * QUARTER, QUARTER), rows((1 - y) * QUARTER, QUARTER)
            k2_a[...] = keep_a[slot, :, mine, :] + r1_a[slot, :, mine, :].astype(F32)
            s2_a[...] = (keep_a[slot, :, theirs, :] + r1_a[slot, :, theirs, :].astype(F32)).astype(BF16)
            a_copy(2, b, s2_a, r2_a.at[slot], to_y).start()

    def tick_b(t):
        @pl.when(live(t, 6))
        def _():
            b = t - 6
            b_copy(7, b, core_of(gb, b, c), core_of(gb, b, c), to_core).wait_send()
            b_copy(7, b, core_of(gb, b, 1 - c), core_of(gb, b, 1 - c), to_core).wait_recv()

        @pl.when(live(t, 5))
        def _():
            b = t - 5
            copy = b_copy(6, b, core_of(gb, b, c), core_of(gb, b, c), to_z)

            @pl.when(inner)
            def _():
                copy.wait_send()

            @pl.when(end)
            def _():
                copy.wait_recv()

            b_copy(7, b, core_of(gb, b, c), core_of(gb, b, c), to_core).start()

        @pl.when(live(t, 4) & inner)
        def _():
            b = t - 4
            b_copy(5, b, g_b, own_b(b), to_mid).wait_send()
            b_copy(5, b, g_b, other_b(b), to_mid).wait_recv()
            pltpu.make_async_copy(g_b, own_b(b), loc_b).wait()
            b_copy(6, b, core_of(gb, b, c), core_of(gb, b, c), to_z).start()

        @pl.when(live(t, 3) & inner)
        def _():
            b = t - 3
            copy = b_copy(4, b, s4_b, r4_b.at[b % 2], to_y)
            copy.wait_send()
            copy.wait_recv()
            g_b[...] = (s4_b[...].astype(F32) + r4_b[b % 2].astype(F32)).astype(BF16)
            pltpu.make_async_copy(g_b, own_b(b), loc_b).start()
            b_copy(5, b, g_b, own_b(b), to_mid).start()

        @pl.when(live(t, 2) & inner)
        def _():
            b = t - 2
            copy = b_copy(3, b, s3_b, r3_b.at[b % 2], to_mid)
            copy.wait_send()
            copy.wait_recv()
            s4_b[...] = (k2_b[...] + r3_b[b % 2].astype(F32)).astype(BF16)
            b_copy(4, b, s4_b, r4_b.at[b % 2], to_y).start()

        @pl.when(live(t, 1))
        def _():
            b = t - 1
            slot = b % SLOTS_B[2]
            copy = b_copy(2, b, s2_b, r2_b.at[slot], to_z)

            @pl.when(end)
            def _():
                copy.wait_send()

            @pl.when(inner)
            def _():
                copy.wait_recv()
                mine, theirs = rows(high * QUARTER, QUARTER), rows((1 - high) * QUARTER, QUARTER)
                k2_b[...] = acc1_b[:, mine, :] + r2_b[slot, :, mine, :].astype(F32)
                s3_b[...] = (acc1_b[:, theirs, :] + r2_b[slot, :, theirs, :].astype(F32)).astype(BF16)
                b_copy(3, b, s3_b, r3_b.at[b % 2], to_mid).start()

        @pl.when(live(t, 0))
        def _():
            b = t
            slot = b % 2
            for m in range(3):
                first_b(b, m).wait()
            total = keep_b[slot] + r1_b[slot].astype(F32)

            @pl.when(inner)
            def _():
                acc1_b[...] = total

            @pl.when(end)
            def _():
                s2_b[...] = total.astype(BF16)
                b_copy(2, b, s2_b, r2_b.at[b % SLOTS_B[2]], to_z).start()

    def turn(at, by_a):
        wide = H[at, :].astype(F32)
        scale = scale_of(wide)
        da = by_a.astype(BF16).astype(F32)
        along = jnp.sum(da * wide, -1, keepdims=True) * (scale * scale * scale) * (1.0 / D)
        by_h = (da * scale - wide * along).astype(BF16).astype(F32)
        by_y = (DY[at, :].astype(F32) + by_h).astype(BF16)
        DY[at, :] = by_y
        DT[:, at] = by_y.T

    def gradients(t):
        slot = (t + PER_LAYER) % 2
        layer = 1 - t // PER_LAYER

        def body(at):
            a = P_[layer, at, :]
            gate, up = nn(a, wg_v[slot]), nn(a, wu_v[slot])
            by_hid = nt(DY[at, :], wd_v[slot]).astype(BF16).astype(F32)
            sig = jax.nn.sigmoid(gate)
            act = gate * sig
            HID[at, :] = (act * up).astype(BF16)
            by_gate = (by_hid * up * (sig + act * (1.0 - sig))).astype(BF16)
            by_up = (by_hid * act).astype(BF16)
            DG[at, :] = by_gate
            DU[at, :] = by_up

        tiles(body)

    def by_input(t, then=None):
        slot = (t + PER_LAYER) % 2

        def body(at):
            total = ACC[at, :] + (nt(DG[at, :], wg_v[slot]) + nt(DU[at, :], wu_v[slot]))
            if then is None:
                ACC[at, :] = total
            else:
                then(at, total)

        tiles(body)

    def weights_of(t):
        slot = t % 2
        layer = 1 - t // PER_LAYER
        pairs = ((AT.at[layer], DG), (AT.at[layer], DU), (DT, HID))

        def send(m):
            first_a(t, m).start()
            first_b(t, m).start()

        for m, (left, right) in enumerate(pairs):
            total = nn(left[rows((1 - c) * HALF, HALF), :], right[...]).astype(BF16)
            sb_a[slot, m] = total[:, :LANES]
            sb_b[slot, m] = total[:, LANES:]
            if m:
                send(m - 1)
        for m, (left, right) in enumerate(pairs):
            total = nn(left[rows(c * HALF, HALF), :], right[...])
            keep_a[slot, m] = total[:, :LANES]
            keep_b[slot, m] = total[:, LANES:]
            if m == 0:
                send(2)

    def main(t, carry):
        @pl.when(t < BLOCKS)
        def _():
            arrive(t + PER_LAYER)

            @pl.when(t < BLOCKS - 1)
            def _():
                fetch(t + PER_LAYER + 1)

            gradients(t)

        tick_b(t - 1)

        @pl.when(t < BLOCKS)
        def _():
            weights_of(t)

        @pl.when(t < PER_LAYER - 1)
        def _():
            by_input(t)

        @pl.when(t == PER_LAYER - 1)
        def _():
            by_input(t, turn)

        tick_a(t)
        return carry

    lax.fori_loop(0, BLOCKS + 7, main, 0)


def summed_gradients(x, dy, wg, wu, wd):
    unit = lambda n, height, dtype: pltpu.VMEM((n, 3, height, LANES) if n else (3, height, LANES), dtype)
    scratch = [
        pltpu.VMEM((2, TOKENS, D), BF16),
        pltpu.VMEM((TOKENS, D), BF16),
        pltpu.VMEM((TOKENS, D), BF16),
        pltpu.VMEM((2, D, TOKENS), BF16),
        pltpu.VMEM((D, TOKENS), BF16),
        pltpu.VMEM((TOKENS, D), F32),
        pltpu.VMEM((TOKENS, BLOCK), BF16),
        pltpu.VMEM((TOKENS, BLOCK), BF16),
        pltpu.VMEM((TOKENS, BLOCK), BF16),
        pltpu.VMEM((2, D, BLOCK), BF16),
        pltpu.VMEM((2, D, BLOCK), BF16),
        pltpu.VMEM((2, BLOCK, D), BF16),
        unit(2, HALF, BF16), unit(2, HALF, F32), unit(2, HALF, BF16),
        unit(0, QUARTER, BF16), unit(0, QUARTER, F32), unit(2, QUARTER, BF16),
        unit(0, QUARTER, BF16), unit(0, QUARTER, F32), unit(SLOTS_A[3], QUARTER, BF16),
        unit(0, QUARTER, BF16), unit(2, QUARTER, BF16), unit(0, QUARTER, BF16),
        unit(2, HALF, BF16), unit(2, HALF, F32), unit(2, HALF, BF16),
        unit(0, HALF, BF16), unit(0, HALF, F32), unit(SLOTS_B[2], HALF, BF16),
        unit(0, QUARTER, BF16), unit(0, QUARTER, F32), unit(2, QUARTER, BF16),
        unit(0, QUARTER, BF16), unit(2, QUARTER, BF16), unit(0, QUARTER, BF16),
        pltpu.SemaphoreType.DMA((TOKENS // TILE + 1,)),
        pltpu.SemaphoreType.DMA((2, 3)),
        pltpu.SemaphoreType.DMA,
        pltpu.SemaphoreType.DMA,
        pltpu.SemaphoreType.DMA((2, 2, 3)),
        pltpu.SemaphoreType.DMA((2, 2, 3)),
        pltpu.SemaphoreType.DMA((8,)),
        pltpu.SemaphoreType.DMA((8,)),
        *[pltpu.SemaphoreType.DMA((SLOTS_A[s],)) for s in range(2, 8)],
        *[pltpu.SemaphoreType.DMA((SLOTS_B[s],)) for s in range(2, 8)],
    ]
    out = jax.ShapeDtypeStruct((BLOCKS, 3, D, LANES), BF16)
    return pl.pallas_call(
        step_kernel,
        out_shape=(out, out),
        in_specs=[pl.BlockSpec(memory_space=pl.ANY)] * 5,
        out_specs=(pl.BlockSpec(memory_space=pl.ANY),) * 2,
        scratch_shapes=scratch,
        compiler_params=pltpu.CompilerParams(collective_id=0, has_side_effects=True, vmem_limit_bytes=62 * 2**20),
        name="gradients",
    )(x, dy, wg, wu, wd)


def adamw(w, m, v, g):
    m = 0.9 * m + 0.1 * g
    v = 0.95 * v + 0.05 * g * g
    step = m * lax.rsqrt(v + 1e-8) + 0.1 * w
    return (w - 0.02 * step).astype(BF16), m, v


def update_wide(*refs):
    ins, outs = (refs[:5], refs[5:10]), (refs[10:13], refs[13:])
    for (w_ref, m_ref, v_ref, ga_ref, gb_ref), (w_out, m_out, v_out) in zip(ins, outs, strict=True):
        for j in range(FF // LANES):
            at = slice(j * LANES, (j + 1) * LANES)
            g = (ga_ref, gb_ref)[j % 2][j // 2, 0].astype(F32)
            w_out[0, :, at], m_out[0, :, at], v_out[0, :, at] = adamw(
                w_ref[0, :, at].astype(F32), m_ref[0, :, at], v_ref[0, :, at], g
            )


TALL = 2 * BLOCK


def update_tall(w_ref, m_ref, v_ref, ga_ref, gb_ref, w_out, m_out, v_out):
    for k in range(TALL // LANES):
        at = slice(k * LANES, (k + 1) * LANES)
        g = (ga_ref, gb_ref)[k % 2][k // 2, 0].T.astype(F32)
        w_out[0, at], m_out[0, at], v_out[0, at] = adamw(w_ref[0, at].astype(F32), m_ref[0, at], v_ref[0, at], g)


def new_arrays(shape):
    return [jax.ShapeDtypeStruct(shape, t) for t in (BF16, F32, F32)]


def update_gate_up(gate, up, ga, gb):
    height = 112
    spec = pl.BlockSpec((1, height, FF), lambda l, i: (l, i, 0))

    def g_spec(which):
        return pl.BlockSpec((PER_LAYER, 1, height, LANES), lambda l, i: (1 - l, which, i, 0))

    new = pl.pallas_call(
        update_wide,
        grid=(2, D // height),
        in_specs=[spec] * 3 + [g_spec(0)] * 2 + [spec] * 3 + [g_spec(1)] * 2,
        out_specs=[spec] * 6,
        out_shape=new_arrays(gate[0].shape) * 2,
        compiler_params=pltpu.CompilerParams(vmem_limit_bytes=60 * 2**20),
        name="update_gate_up",
    )(*gate, ga, gb, *up, ga, gb)
    return new[:3], new[3:]


def update_down(down, ga, gb):
    spec = pl.BlockSpec((1, TALL, D), lambda l, i: (l, i, 0))
    g_spec = pl.BlockSpec((TALL // BLOCK, 1, D, LANES), lambda l, i: ((1 - l) * (FF // TALL) + i, 2, 0, 0))
    return pl.pallas_call(
        update_tall,
        grid=(2, FF // TALL),
        in_specs=[spec] * 3 + [g_spec] * 2,
        out_specs=[spec] * 3,
        out_shape=new_arrays(down[0].shape),
        compiler_params=pltpu.CompilerParams(vmem_limit_bytes=60 * 2**20),
        name="update_down",
    )(*down, ga, gb)


def solution(mesh):
    def step(x, dy, *arrays):
        weights, m, v = (arrays[i : i + 3] for i in (0, 3, 6))
        ga, gb = summed_gradients(x, dy, *weights)
        gate, up, down = zip(weights, m, v, strict=True)
        new = [*update_gate_up(gate, up, ga, gb), update_down(down, ga, gb)]
        return tuple(one[which] for which in range(3) for one in new)

    return jax.shard_map(
        step,
        mesh=mesh,
        in_specs=(P(("rep", "dp"), None, None),) * 2 + (P(None, None, None),) * 9,
        out_specs=(P("rep", None, None),) * 9,
        check_vma=False,
    )
```

time: 461 us -> 424 us (0.920)
  Pallas kernels: 460 us -> 423 us
    pallas_call x1, Pallas kernels: 347 us -> 323 us  [summed_gradients(): pl.pallas_call(step_kernel, out_shape=(out, out), in_specs=[pl.BlockSpec(...]
    pallas_call x3 -> x2, Pallas kernels: 113 us -> 99.7 us  [the longest x1 64.9 us: update_gate_up(): pl.pallas_call(update_wide, grid=(2, D // height), in_specs=[spec] * 3 +...]
where the time goes in v2:
time: 424 us; the launch traced here: 423 us
  Pallas kernels  423 us (100%)
    pallas_call x1, Pallas kernels, summed_gradients(): pl.pallas_call(step_kernel, out_shape=(out, out), in_specs=[pl.BlockSpec(...  323 us
    pallas_call x1, Pallas kernels, update_gate_up(): pl.pallas_call(update_wide, grid=(2, D // height), in_specs=[spec] * 3 +...  64.9 us
    pallas_call x1, Pallas kernels, update_down(): pl.pallas_call(update_tall, grid=(2, FF // TALL), in_specs=[spec] * 3 + [...  34.7 us

profile of v2, /device:TPU:0, one launch (start us, length us, event | category | flops | bytes accessed | tf_op | source)
XLA Modules:
  0.0 423.4 jit_solution(8903658401619001794)
XLA Ops:
  0.6 322.9 %gradients.1 = (bf16[20,3,896,128]{3,2,1,0:T(8,128)(2,1)}, bf16[20,3,896,128]{3,2,1,0:T(8,128)(2,1)}) custom-call(bf16[1,2048,896]{2,1,0:T(8,128)(2,1)} %x_hbm.1, bf16[1,2048,896]{2,1,0:T(8,128)(2,1)} %dy_hbm.1, bf16[2,896,2560]{2,1,0:T(8,128)(2,1)} %refs_0_.1, bf16[2,896,2560]{2,1,0:T(8,128)(2,1)} %refs_5_.1, bf16[2,2560,896]{2,1,0:T(8,128)(2,1)} %w_ref.1), custom_call_target="tpu_custom_call" | custom-call | tf_op jit(solution)/shard_map/gradients/pallas_call | solution.py:492
  323.6 34.7 %update_down.1 = (bf16[2,2560,896]{2,1,0:T(8,128)(2,1)}, f32[2,2560,896]{2,1,0:T(8,128)}, f32[2,2560,896]{2,1,0:T(8,128)}) custom-call(bf16[2,2560,896]{2,1,0:T(8,128)(2,1)} %w_ref.1, f32[2,2560,896]{2,1,0:T(8,128)} %m_ref.1, f32[2,2560,896]{2,1,0:T(8,128)} %v_ref.1, bf16[20,3,896,128]{3,2,1,0:T(8,128)(2,1)} %get-tuple-element.20.refs_3_.refs_8_.ga_ref, ...), custom_call_target="tpu_custom_call" | custom-call | tf_op jit(solution)/shard_map/update_down/pallas_call | solution.py:557
  358.3 64.9 %update_gate_up.1 = (bf16[2,896,2560]{2,1,0:T(8,128)(2,1)}, f32[2,896,2560]{2,1,0:T(8,128)}, f32[2,896,2560]{2,1,0:T(8,128)}, bf16[2,896,2560]{2,1,0:T(8,128)(2,...) custom-call(bf16[2,896,2560]{2,1,0:T(8,128)(2,1)} %refs_0_.1, f32[2,896,2560]{2,1,0:T(8,128)} %refs_1_.1, ...), custom_call_target="tpu_custom_call" | custom-call | tf_op jit(solution)/shard_map/update_gate_up/pallas_call | solution.py:542

commit v3 on v2

--- a/solution.py
+++ b/solution.py
@@ -37,7 +37,7 @@
 def step_kernel(x_hbm, dy_hbm, wg_hbm, wu_hbm, wd_hbm, ga, gb, P_, H, DY, AT, DT, ACC, HID, DG, DU, wg_v, wu_v, wd_v, *comm):
     (sb_a, keep_a, r1_a, s2_a, k2_a, r2_a, s3_a, acc_a, r3_a, s4_a, r4_a, g_a,
      sb_b, keep_b, r1_b, s2_b, acc1_b, r2_b, s3_b, k2_b, r3_b, s4_b, r4_b, g_b,
-     load_sem, w_sem, loc_a, loc_b, first_send, first_recv, send_a, send_b, *recvs) = comm
+     load_sem, w_sem, loc_a, loc_b, first_send, first_recv, early_recv, send_a, send_b, *recvs) = comm
     recv_a = dict(zip(range(2, 8), recvs[:6], strict=True))
     recv_b = dict(zip(range(2, 8), recvs[6:], strict=True))
     me = lax.axis_index("dp")
@@ -277,7 +277,13 @@
             s2_a[...] = (keep_a[slot, :, theirs, :] + r1_a[slot, :, theirs, :].astype(F32)).astype(BF16)
             a_copy(2, b, s2_a, r2_a.at[slot], to_y).start()
 
-    def tick_b(t):
+    def out_own(b):
+        return remote(g_b, own_b(b), send_b.at[0], early_recv.at[b % SLOTS_B[6]], to_z)
+
+    def out_other(b):
+        return b_copy(6, b, other_b(b), other_b(b), to_z)
+
+    def late_b(t):
         @pl.when(live(t, 6))
         def _():
             b = t - 6
@@ -287,15 +293,15 @@
         @pl.when(live(t, 5))
         def _():
             b = t - 5
-            copy = b_copy(6, b, core_of(gb, b, c), core_of(gb, b, c), to_z)
 
             @pl.when(inner)
             def _():
-                copy.wait_send()
+                out_other(b).wait_send()
 
             @pl.when(end)
             def _():
-                copy.wait_recv()
+                out_own(b).wait_recv()
+                out_other(b).wait_recv()
 
             b_copy(7, b, core_of(gb, b, c), core_of(gb, b, c), to_core).start()
 
@@ -304,8 +310,13 @@
             b = t - 4
             b_copy(5, b, g_b, own_b(b), to_mid).wait_send()
             b_copy(5, b, g_b, other_b(b), to_mid).wait_recv()
+            out_other(b).start()
             pltpu.make_async_copy(g_b, own_b(b), loc_b).wait()
-            b_copy(6, b, core_of(gb, b, c), core_of(gb, b, c), to_z).start()
+
+    def tick_b(t):
+        @pl.when(live(t, 4) & inner)
+        def _():
+            out_own(t - 4).wait_send()
 
         @pl.when(live(t, 3) & inner)
         def _():
@@ -316,6 +327,7 @@
             g_b[...] = (s4_b[...].astype(F32) + r4_b[b % 2].astype(F32)).astype(BF16)
             pltpu.make_async_copy(g_b, own_b(b), loc_b).start()
             b_copy(5, b, g_b, own_b(b), to_mid).start()
+            out_own(b).start()
 
         @pl.when(live(t, 2) & inner)
         def _():
@@ -448,10 +460,11 @@
         def _():
             by_input(t, turn)
 
+        late_b(t)
         tick_a(t)
         return carry
 
-    lax.fori_loop(0, BLOCKS + 7, main, 0)
+    lax.fori_loop(0, BLOCKS + 6, main, 0)
 
 
 def summed_gradients(x, dy, wg, wu, wd):
@@ -483,6 +496,7 @@
         pltpu.SemaphoreType.DMA,
         pltpu.SemaphoreType.DMA((2, 2, 3)),
         pltpu.SemaphoreType.DMA((2, 2, 3)),
+        pltpu.SemaphoreType.DMA((SLOTS_B[6],)),
         pltpu.SemaphoreType.DMA((8,)),
         pltpu.SemaphoreType.DMA((8,)),
         *[pltpu.SemaphoreType.DMA((SLOTS_A[s],)) for s in range(2, 8)],
@@ -518,7 +532,8 @@
             )
 
 
-TALL = 2 * BLOCK
+TALL = BLOCK
+WIDE = 112
 
 
 def update_tall(w_ref, m_ref, v_ref, ga_ref, gb_ref, w_out, m_out, v_out):
@@ -528,41 +543,35 @@
         w_out[0, at], m_out[0, at], v_out[0, at] = adamw(w_ref[0, at].astype(F32), m_ref[0, at], v_ref[0, at], g)
 
 
-def new_arrays(shape):
-    return [jax.ShapeDtypeStruct(shape, t) for t in (BF16, F32, F32)]
-
-
-def update_gate_up(gate, up, ga, gb):
-    height = 112
-    spec = pl.BlockSpec((1, height, FF), lambda l, i: (l, i, 0))
-
-    def g_spec(which):
-        return pl.BlockSpec((PER_LAYER, 1, height, LANES), lambda l, i: (1 - l, which, i, 0))
-
+def update_all(*refs):
+    @pl.when(pl.program_id(1) < D // WIDE)
+    def _():
+        update_wide(*refs[:10], *refs[15:21])
+
+    update_tall(*refs[10:15], *refs[21:])
+
+
+def update(gate, up, down, ga, gb):
+    last = D // WIDE - 1
+    wide = pl.BlockSpec((1, WIDE, FF), lambda l, i: (l, jnp.minimum(i, last), 0))
+    tall = pl.BlockSpec((1, TALL, D), lambda l, i: (l, i, 0))
+
+    def g_wide(which):
+        return pl.BlockSpec((PER_LAYER, 1, WIDE, LANES), lambda l, i: (1 - l, which, jnp.minimum(i, last), 0))
+
+    g_tall = pl.BlockSpec((1, 1, D, LANES), lambda l, i: ((1 - l) * PER_LAYER + i, 2, 0, 0))
     new = pl.pallas_call(
-        update_wide,
-        grid=(2, D // height),
-        in_specs=[spec] * 3 + [g_spec(0)] * 2 + [spec] * 3 + [g_spec(1)] * 2,
-        out_specs=[spec] * 6,
-        out_shape=new_arrays(gate[0].shape) * 2,
+        update_all,
+        grid=(2, PER_LAYER),
+        in_specs=[wide] * 3 + [g_wide(0)] * 2 + [wide] * 3 + [g_wide(1)] * 2 + [tall] * 3 + [g_tall] * 2,
+        out_specs=[wide] * 6 + [tall] * 3,
+        out_shape=[
+            jax.ShapeDtypeStruct(w.shape, t) for w in (gate[0], up[0], down[0]) for t in (BF16, F32, F32)
+        ],
         compiler_params=pltpu.CompilerParams(vmem_limit_bytes=60 * 2**20),
-        name="update_gate_up",
-    )(*gate, ga, gb, *up, ga, gb)
-    return new[:3], new[3:]
-
-
-def update_down(down, ga, gb):
-    spec = pl.BlockSpec((1, TALL, D), lambda l, i: (l, i, 0))
-    g_spec = pl.BlockSpec((TALL // BLOCK, 1, D, LANES), lambda l, i: ((1 - l) * (FF // TALL) + i, 2, 0, 0))
-    return pl.pallas_call(
-        update_tall,
-        grid=(2, FF // TALL),
-        in_specs=[spec] * 3 + [g_spec] * 2,
-        out_specs=[spec] * 3,
-        out_shape=new_arrays(down[0].shape),
-        compiler_params=pltpu.CompilerParams(vmem_limit_bytes=60 * 2**20),
-        name="update_down",
-    )(*down, ga, gb)
+        name="update",
+    )(*gate, ga, gb, *up, ga, gb, *down, ga, gb)
+    return new[:3], new[3:6], new[6:]
 
 
 def solution(mesh):
@@ -570,7 +579,7 @@
         weights, m, v = (arrays[i : i + 3] for i in (0, 3, 6))
         ga, gb = summed_gradients(x, dy, *weights)
         gate, up, down = zip(weights, m, v, strict=True)
-        new = [*update_gate_up(gate, up, ga, gb), update_down(down, ga, gb)]
+        new = update(gate, up, down, ga, gb)
         return tuple(one[which] for which in range(3) for one in new)
 
     return jax.shard_map(

time: 424 us -> 417 us (0.983)
  Pallas kernels: 423 us -> 416 us
    pallas_call x2 -> x1, Pallas kernels: 99.7 us -> 96.7 us  [update(): pl.pallas_call(update_all, grid=(2, PER_LAYER), in_specs=[wide] * 3 + [g_...]
where the time goes in v3:
time: 417 us
  Pallas kernels  416 us (100%)
    pallas_call x1, Pallas kernels, summed_gradients(): pl.pallas_call(step_kernel, out_shape=(out, out), in_specs=[pl.BlockSpec(...  320 us
    pallas_call x1, Pallas kernels, update(): pl.pallas_call(update_all, grid=(2, PER_LAYER), in_specs=[wide] * 3 + [g_...  96.7 us

profile of v3, /device:TPU:0, one launch (start us, length us, event | category | flops | bytes accessed | tf_op | source)
XLA Modules:
  0.0 417.2 jit_solution(12621071682102870466)
XLA Ops:
  0.6 319.7 %gradients.1 = (bf16[20,3,896,128]{3,2,1,0:T(8,128)(2,1)}, bf16[20,3,896,128]{3,2,1,0:T(8,128)(2,1)}) custom-call(bf16[1,2048,896]{2,1,0:T(8,128)(2,1)} %x_hbm.1, bf16[1,2048,896]{2,1,0:T(8,128)(2,1)} %dy_hbm.1, bf16[2,896,2560]{2,1,0:T(8,128)(2,1)} %refs_0_.1, bf16[2,896,2560]{2,1,0:T(8,128)(2,1)} %refs_5_.1, bf16[2,2560,896]{2,1,0:T(8,128)(2,1)} %refs_10_.1), custom_call_target="tpu_custom_call" | custom-call | tf_op jit(solution)/shard_map/gradients/pallas_call | solution.py:506
  320.3 96.7 %update.1 = (bf16[2,896,2560]{2,1,0:T(8,128)(2,1)}, f32[2,896,2560]{2,1,0:T(8,128)}, f32[2,896,2560]{2,1,0:T(8,128)}, bf16[2,896,2560]{2,1,0:T(8,128)(2,1)}, f32...) custom-call(bf16[2,896,2560]{2,1,0:T(8,128)(2,1)} %refs_0_.1, ...), custom_call_target="tpu_custom_call" | custom-call | tf_op jit(solution)/shard_map/update/pallas_call | solution.py:563
